TPU v7x, 256 devices: a whole 4x4x8 slice. The times are simulated.
256 devices in a mesh: mb: 8 (over z), tp: 8 (over y, core), dp: 4 (over x).
Axes of the slice: x: 4, y: 4, z: 8, core: 2. Of those that a mesh axis runs over, the one named last changes fastest.
Arguments:
- hidden: bfloat16 [4, 16, 512, 7168], P('dp', 'mb', None, 'tp'), may hold values from -6 to 6
- latent: bfloat16 [4, 16, 512, 512], P('dp', 'mb', None, 'tp'), may hold values from -6 to 6
- out_grad: bfloat16 [4, 16, 512, 16384], P('dp', 'mb', None, 'tp'), may hold values from -0.059814453 to 0.059814453
- up_weight: bfloat16 [512, 16384], P(None, 'tp'), may hold values from -0.046875 to 0.046875
- mb_tokens: int32 [4, 16], P('dp'), may hold values from 128 to 512, as said below
- slot_mb: int32 [4, 16], P('dp', 'mb'), may hold values from 0 to 15, each once within a row
Outputs:
- up_grad: float32 [512, 16384], P(('mb', 'dp'), 'tp')
- running_down: float32 [8, 7168, 512], P('mb', 'tp', 'dp')
Inputs may be any that keep to these rules, and one draw needn't show every extreme that they name: `mb_tokens`: each count is a multiple of 128; in every group some microbatch has exactly 512 tokens. `slot_mb`: each row is a permutation of the microbatch numbers.
All inputs are finite; a program needn't handle non-finite values.
Results may differ from a plain program's by a relative error of at most 0.005.
Values may be sent and summed in bfloat16 or wider, within the bound.
A program may use at most 128 MiB of HBM per device.

v0:
```python
import jax
import jax.numpy as jnp
from jax import lax
from jax.sharding import PartitionSpec as P


def copy_for_each(value, axis):
    copies = jnp.broadcast_to(value, (lax.axis_size(axis), *value.shape))
    return lax.all_to_all(copies, axis, split_axis=0, concat_axis=0, tiled=True)


def laid_out(blocks, dim):
    blocks = jnp.moveaxis(blocks, 0, dim)
    dims = blocks.shape
    return blocks.reshape(*dims[:dim], dims[dim] * dims[dim + 1], *dims[dim + 2 :])


def gathered_copies(value, axis, dim):
    blocks = copy_for_each(value, axis)
    return laid_out(blocks, dim)


def rows_for(lines, length):
    spare = -lines.shape[0] % length
    if not spare:
        return lines
    return jnp.concatenate([lines, jnp.zeros((spare, *lines.shape[1:]), lines.dtype)])


def total_of(value, axis):
    lines = value.reshape(-1, *value.shape[1:][-1:])
    padded = rows_for(lines, lax.axis_size(axis))
    own = lax.psum_scatter(padded, axis, scatter_dimension=0, tiled=True)
    whole = lax.all_gather(own, axis, axis=0, tiled=True)
    return whole[: len(lines)].reshape(value.shape)


def split_up(value, dim, length):
    dims = value.shape
    blocks = value.reshape(*dims[:dim], length, dims[dim] // length, *dims[dim + 1 :])
    return jnp.moveaxis(blocks, dim, 0)


def summed_on_arrival(value, axis, dim):
    blocks = split_up(value, dim, lax.axis_size(axis))
    arrived = lax.all_to_all(blocks, axis, split_axis=0, concat_axis=0, tiled=True)
    return arrived.sum(axis=0)


def local(hidden, latent, out_grad, up_weight, mb_tokens, slot_mb):
    slot_count = hidden.shape[1]
    capacity = hidden.shape[2]
    micro_count = mb_tokens.shape[1]
    row_total = slot_count * capacity
    slot_ids = slot_mb[0]
    lookup = slot_ids[:, None] == jnp.arange(micro_count, dtype=jnp.int32)[None, :]
    counts = jnp.sum(jnp.where(lookup, mb_tokens[0][None, :], 0), axis=1)
    valid_rows = jnp.arange(capacity, dtype=jnp.int32)[None, :] < counts[:, None]
    masked_grads = jnp.where(valid_rows[:, :, None], out_grad[0], jnp.zeros((), out_grad.dtype))
    masked_grads = masked_grads.reshape(row_total, -1)
    factors = gathered_copies(latent[0].reshape(row_total, -1), "tp", 1)
    partial_latent = lax.dot_general(
        masked_grads, up_weight, (((1,), (1,)), ((), ())), preferred_element_type=jnp.float32
    )
    latent_grad = total_of(partial_latent, "tp").astype(jnp.bfloat16)
    owner_part = lax.psum_scatter(
        lax.dot_general(
            factors, masked_grads, (((0,), (0,)), ((), ())), preferred_element_type=jnp.float32
        ),
        "mb",
        scatter_dimension=0,
        tiled=True,
    )
    up_grad = summed_on_arrival(owner_part, "dp", 0)
    hidden_rows = hidden[0].reshape(row_total, -1)
    down_term = lax.dot_general(
        hidden_rows, latent_grad, (((0,), (0,)), ((), ())), preferred_element_type=jnp.float32
    )
    down_share = summed_on_arrival(down_term, "dp", 1)
    own_index = lax.axis_index("mb")
    shard_rows = lax.all_gather(down_share[None], "mb", axis=0, tiled=True)
    positions = jnp.arange(shard_rows.shape[0], dtype=jnp.int32)
    weights_in = (positions <= own_index).astype(jnp.float32)
    running = jnp.einsum("k,kdr->dr", weights_in, shard_rows)
    return (up_grad, running[None])


def solution(mesh):
    return jax.shard_map(
        local,
        mesh=mesh,
        in_specs=(
            P("dp", "mb", None, "tp"),
            P("dp", "mb", None, "tp"),
            P("dp", "mb", None, "tp"),
            P(None, "tp"),
            P("dp", None),
            P("dp", "mb"),
        ),
        out_specs=(P(("mb", "dp"), "tp"), P("mb", "tp", "dp")),
        check_vma=False,
    )
```

profile of v0, /device:TPU:4, one launch (start us, length us, event | category | flops | bytes accessed | tf_op | source)
XLA Modules:
  0.0 198.9 jit_solution(7407583883337681670)
XLA Ops:
  8.0 0.0 copy-start
  8.0 0.0 reduce-scatter.5.cloned.1.call-start
  8.1 1.0 fusion.5
  9.1 0.1 iota_compare_fusion
  9.2 2.5 %bitcast_select_fusion = bf16[1024,2048]{1,0:T(8,128)(2,1)S(1)} fusion(bf16[1,2,512,2048]{3,2,1,0:T(8,128)(2,1)} %param.8, pred[1024]{0:T(1024)(128)(4,1)S(1)} %lt.24), kind=kLoop, calls=%fused_computation | loop fusion | flops 2097152 | bytes 8389632 | tf_op jit(solution)/shard_map/jit(_where)/select_n | solution.py:59
  11.7 0.0 copy-done
  11.7 3.7 %fusion.8 = f32[1024,512]{1,0:T(8,128)} fusion(bf16[1024,2048]{1,0:T(8,128)(2,1)S(1)} %bitcast_select_fusion, bf16[512,2048]{1,0:T(8,128)(2,1)S(1)} %copy-done), kind=kOutput, calls=%fused_computation.13 | convolution fusion | flops 2147483648 | bytes 8388608 | tf_op jit(solution)/shard_map/dot_general | solution.py:62
  15.4 0.0 copy-start.1
  15.4 0.0 reduce-scatter.5.cloned.1.call-update
  15.5 0.0 all-gather.4.cloned.1.call-start
  15.5 39.4 %reduce-scatter.5.cloned.1.call-done = f32[128,512]{1,0:T(8,128)} async-done(((f32[1024,512]{1,0:T(8,128)}), f32[128,512]{1,0:T(8,128)}) %reduce-scatter.5.cloned.1.call-update) | async-done | bytes 262160 | tf_op jit(solution)/shard_map/reduce_scatter | solution.py:33
  55.0 0.0 all-gather.4.cloned.1.call-update
  55.0 0.0 copy-done.1
  55.0 0.1 copy.12
  55.2 1.1 broadcast_in_dim.48
  56.3 3.6 %all-to-all-start = ((bf16[8,1024,64]{1,2,0:T(8,128)(2,1)}), bf16[8,1024,64]{1,2,0:T(8,128)(2,1)S(1)}, u32[]{:S(2)}, u32[]{:S(2)}) async-start(bf16[8,1024,64]{1,2,0:T(8,128)(2,1)} %broadcast_in_dim.48), calls=%async_computation | async-start | bytes 2097152 | tf_op jit(solution)/shard_map/all_to_all | solution.py:9
  59.8 0.0 reduce-scatter.7.cloned.1.call-start
  59.9 4.5 %broadcast_select_fusion = bf16[1,2,512,2048]{3,2,1,0:T(8,128)(2,1)} fusion(bf16[1,2,512,2048]{3,2,1,0:T(8,128)(2,1)} %param.8, pred[2,512]{1,0:T(4,128)(4,1)S(1)} %iota_compare_fusion), kind=kLoop, calls=%fused_computation.1 | loop fusion | flops 2097152 | bytes 8389632 | tf_op jit(solution)/shard_map/jit(_where)/select_n | solution.py:59
  64.4 15.6 %all-to-all-done = bf16[8,1024,64]{1,2,0:T(8,128)(2,1)S(1)} async-done(((bf16[8,1024,64]{1,2,0:T(8,128)(2,1)}), bf16[8,1024,64]{1,2,0:T(8,128)(2,1)S(1)}, u32[]{:S(2)}, u32[]{:S(2)}) %all-to-all-start) | async-done | bytes 1048608 | tf_op jit(solution)/shard_map/all_to_all | solution.py:9
  80.0 6.6 %convolution_bitcast_fusion = f32[512,2048]{0,1:T(8,128)} fusion(bf16[1024,2048]{1,0:T(8,128)(2,1)} %bitcast.38, bf16[1024,512]{0,1:T(8,128)(2,1)S(1)} %bitcast.41), kind=kOutput, calls=%fused_computation.2 | convolution fusion | flops 2147483648 | bytes 9437184 | tf_op jit(solution)/shard_map/dot_general | solution.py:67
  86.6 5.4 %copy.15 = f32[512,2048]{1,0:T(8,128)} copy(f32[512,2048]{0,1:T(8,128)} %convolution_bitcast_fusion) | data formatting | bytes 8388608
  92.0 0.0 reduce-scatter.7.cloned.1.call-update
  92.0 0.0 all-gather.6.cloned.1.call-start
  92.1 0.0 all-gather.4.cloned.1.call-done
  92.1 3.4 %fusion = f32[512,896]{1,0:T(8,128)S(1)} fusion(bf16[1024,896]{1,0:T(8,128)(2,1)} %bitcast.45, f32[1024,512]{1,0:T(8,128)} %all-gather.4.cloned.1.call-done), kind=kOutput, calls=%fused_computation.3 | convolution fusion | flops 940048384 | bytes 5767168 | tf_op jit(solution)/shard_map/dot_general | solution.py:76
  95.5 24.0 %all_to_all.15 = f32[4,896,128]{1,2,0:T(8,128)} all-to-all(f32[4,896,128]{1,2,0:T(8,128)S(1)} %bitcast.40), channel_id=1, replica_groups=mesh['mb'=8,'tp'=8,'dp'=4] {'dp'}, dimensions={0} | all-to-all | bytes 3670016 | tf_op jit(solution)/shard_map/all_to_all | solution.py:46
  119.5 2.4 %reduce_sum.29 = bf16[896,128]{0,1:T(8,128)(2,1)} reduce(f32[4,896,128]{1,2,0:T(8,128)} %all_to_all.15, f32[]{:T(128)} %constant.4.clone.1), dimensions={0}, to_apply=%region_4.5 | reduce | flops 344064 | bytes 2064388 | tf_op jit(solution)/shard_map/reduce_sum | solution.py:47
  121.9 0.0 all-gather.6.cloned.1.call-update
  122.0 24.7 %reduce-scatter.7.cloned.1.call-done = f32[64,2048]{1,0:T(8,128)} async-done(((f32[512,2048]{1,0:T(8,128)}), f32[64,2048]{1,0:T(8,128)}) %reduce-scatter.7.cloned.1.call-update) | async-done | bytes 524304 | tf_op jit(solution)/shard_map/reduce_scatter | solution.py:66
  146.7 4.8 %all-to-all-start.1 = ((f32[4,16,2048]{2,1,0:T(8,128)}), f32[4,16,2048]{2,1,0:T(8,128)S(1)}, u32[]{:S(2)}, u32[]{:S(2)}) async-start(f32[4,16,2048]{2,1,0:T(8,128)} %bitcast.43), calls=%async_computation.1 | async-start | bytes 1048576 | tf_op jit(solution)/shard_map/all_to_all | solution.py:46
  151.5 6.4 %all-to-all-done.1 = f32[4,16,2048]{2,1,0:T(8,128)S(1)} async-done(((f32[4,16,2048]{2,1,0:T(8,128)}), f32[4,16,2048]{2,1,0:T(8,128)S(1)}, u32[]{:S(2)}, u32[]{:S(2)}) %all-to-all-start.1) | async-done | bytes 524320 | tf_op jit(solution)/shard_map/all_to_all | solution.py:46
  157.8 0.7 reduce_sum.28
  158.5 29.4 %all-gather.6.cloned.1.call-done = bf16[7168,128]{0,1:T(8,128)(2,1)} async-done(((bf16[896,128]{0,1:T(8,128)(2,1)}), bf16[7168,128]{0,1:T(8,128)(2,1)}) %all-gather.6.cloned.1.call-update) | async-done | bytes 1835024 | tf_op jit(solution)/shard_map/all_gather | solution.py:81
  187.9 1.8 copy.18
  189.7 0.6 fusion.2
  190.4 1.1 copy.14
  (2 shorter events, 0.0 us)
Async XLA Ops:
  8.0 3.7 %copy-start = (bf16[512,2048]{1,0:T(8,128)(2,1)S(1)}, bf16[512,2048]{1,0:T(8,128)(2,1)}, u32[]{:S(2)}) copy-start(bf16[512,2048]{1,0:T(8,128)(2,1)} %param.9) | copy-start | bytes 6291460
  8.0 46.9 %reduce-scatter.5.cloned.1.call-start = ((), (), s32[]{:S(2)}) async-start(), calls=%async_computation.5 | async-start | bytes 2359296 | tf_op jit(solution)/shard_map/reduce_scatter | solution.py:33
  15.4 39.5 %copy-start.1 = (bf16[1,2,512,64]{2,3,1,0:T(8,128)(2,1)S(1)}, bf16[1,2,512,64]{2,3,1,0:T(8,128)(2,1)}, u32[]{:S(2)}) copy-start(bf16[1,2,512,64]{2,3,1,0:T(8,128)(2,1)} %param.7) | copy-start | bytes 393220
  15.5 76.6 %all-gather.4.cloned.1.call-start = ((), (), s32[]{:S(2)}) async-start(), calls=%async_computation.6 | async-start | bytes 2359296 | tf_op jit(solution)/shard_map/all_gather | solution.py:34
  56.3 23.7 %all-to-all-start = ((bf16[8,1024,64]{1,2,0:T(8,128)(2,1)}), bf16[8,1024,64]{1,2,0:T(8,128)(2,1)S(1)}, u32[]{:S(2)}, u32[]{:S(2)}) async-start(bf16[8,1024,64]{1,2,0:T(8,128)(2,1)} %broadcast_in_dim.48), calls=%async_computation | async-start | bytes 2097152 | tf_op jit(solution)/shard_map/all_to_all | solution.py:9
  59.8 86.8 %reduce-scatter.7.cloned.1.call-start = ((), (), s32[]{:S(2)}) async-start(), calls=%async_computation.8 | async-start | bytes 4718592 | tf_op jit(solution)/shard_map/reduce_scatter | solution.py:66
  92.0 95.9 %all-gather.6.cloned.1.call-start = ((), (), s32[]{:S(2)}) async-start(), calls=%async_computation.7 | async-start | bytes 2064384 | tf_op jit(solution)/shard_map/all_gather | solution.py:81
  146.7 11.2 %all-to-all-start.1 = ((f32[4,16,2048]{2,1,0:T(8,128)}), f32[4,16,2048]{2,1,0:T(8,128)S(1)}, u32[]{:S(2)}, u32[]{:S(2)}) async-start(f32[4,16,2048]{2,1,0:T(8,128)} %bitcast.43), calls=%async_computation.1 | async-start | bytes 1048576 | tf_op jit(solution)/shard_map/all_to_all | solution.py:46
Sparse Core Ops, SparseCore 0:
  15.6 39.3 reduce-scatter.4
  56.8 28.7 all-gather.3
Sparse Core Ops, SparseCore 1:
  92.1 54.5 reduce-scatter.6
  148.9 38.9 all-gather.5
where the time goes:
time: 199 us
  waiting for transfers between devices  116 us (58%)
  blocking collectives  24 us (12%)
  between operations  15.6 us (8%)
  matrix products  14.4 us (7%)
  other arithmetic  11.2 us (6%)
  local copies, waits for them, and re-layouts  9.6 us (5%)
  starting transfers between devices  8.52 us (4%)
    reduce_scatter x1, waiting for transfers between devices, total_of(): own = lax.psum_scatter(padded, axis, scatter_dimension=0, tiled=True)  39.4 us
    all_gather x1, waiting for transfers between devices, local(): shard_rows = lax.all_gather(down_share[None], 'mb', axis=0, tiled=True)  29.4 us
    reduce_scatter x1, waiting for transfers between devices, local(): lax.psum_scatter(lax.dot_general(factors, masked_grads, (((0,), (0,)), ((...  24.7 us
    all_to_all x1, blocking collectives, summed_on_arrival(): lax.all_to_all(blocks, axis, split_axis=0, concat_axis=0, tiled=True)  24 us
    all_to_all x1, waiting for transfers between devices, copy_for_each(): return lax.all_to_all(copies, axis, split_axis=0, concat_axis=0, tiled=True)  15.6 us
    unnamed x8, local copies, waits for them, and re-layouts  7.35 us
    select_n x2, other arithmetic, local(): jnp.where(valid_rows[:, :, None], out_grad[0], jnp.zeros((), out_grad.dty...  7.03 us
    dot_general x1, matrix products, local(): lax.dot_general(factors, masked_grads, (((0,), (0,)), ((), ())), preferre...  6.64 us
  transfers between devices with their start and end apart: 6, of which 5 were waited for; matrix products, arithmetic and copies ran while one was open for 12% of the time, Pallas kernels for 0%

commit v1 on v0

--- a/solution.py
+++ b/solution.py
@@ -78,7 +78,9 @@
     )
     down_share = summed_on_arrival(down_term, "dp", 1)
     own_index = lax.axis_index("mb")
-    shard_rows = lax.all_gather(down_share[None], "mb", axis=0, tiled=True)
+    shard_rows = jnp.concatenate(
+        lax.all_to_all(jnp.stack([down_share[None]] * lax.axis_size("mb")), "mb", 0, 0), axis=0
+    )
     positions = jnp.arange(shard_rows.shape[0], dtype=jnp.int32)
     weights_in = (positions <= own_index).astype(jnp.float32)
     running = jnp.einsum("k,kdr->dr", weights_in, shard_rows)

time: 199 us -> 223 us (1.12); the launches traced: 199 us -> 219 us
  waiting for transfers between devices: 116 us -> 131 us
  starting transfers between devices: 8.52 us -> 12.8 us
  matrix products: 14.4 us -> 17.3 us
    all_to_all x0 -> x1, waiting for transfers between devices: none -> 43.9 us  [local(): lax.all_to_all(jnp.stack([down_share[None]] * lax.axis_size('mb')), 'mb',...]
    all_gather x1 -> x0, waiting for transfers between devices: 29.4 us -> none  [local(): shard_rows = lax.all_gather(down_share[None], 'mb', axis=0, tiled=True)]
    all_to_all x0 -> x1, starting transfers between devices: none -> 4.36 us  [local(): lax.all_to_all(jnp.stack([down_share[None]] * lax.axis_size('mb')), 'mb',...]
    dot_general x1, matrix products: 0.62 us -> 3.51 us  [local(): running = jnp.einsum('k,kdr->dr', weights_in, shard_rows)]
    reduce_scatter x1, waiting for transfers between devices: 24.7 us -> 27.1 us  [local(): lax.psum_scatter(lax.dot_general(factors, masked_grads, (((0,), (0,)), ((...]
    unnamed x8 -> x7, local copies, waits for them, and re-layouts: 7.35 us -> 5.56 us
  transfers between devices with their start and end apart: 6 -> 6, of which waited for: 5 -> 5; matrix products, arithmetic and copies ran while one was open for 12% -> 11% of each run, Pallas kernels for 0% -> 0%
where the time goes in v1:
time: 223 us; the launch traced here: 219 us
  waiting for transfers between devices  131 us (59%)
  blocking collectives  24.1 us (11%)
  matrix products  17.3 us (8%)
  between operations  15.6 us (7%)
  starting transfers between devices  12.8 us (6%)
  other arithmetic  10.4 us (5%)
  local copies, waits for them, and re-layouts  8.32 us (4%)
    all_to_all x1, waiting for transfers between devices, local(): lax.all_to_all(jnp.stack([down_share[None]] * lax.axis_size('mb')), 'mb',...  43.9 us
    reduce_scatter x1, waiting for transfers between devices, total_of(): own = lax.psum_scatter(padded, axis, scatter_dimension=0, tiled=True)  39.4 us
    reduce_scatter x1, waiting for transfers between devices, local(): lax.psum_scatter(lax.dot_general(factors, masked_grads, (((0,), (0,)), ((...  27.1 us
    all_to_all x1, blocking collectives, summed_on_arrival(): lax.all_to_all(blocks, axis, split_axis=0, concat_axis=0, tiled=True)  24.1 us
    all_to_all x1, waiting for transfers between devices, copy_for_each(): return lax.all_to_all(copies, axis, split_axis=0, concat_axis=0, tiled=True)  15.6 us
    select_n x2, other arithmetic, local(): jnp.where(valid_rows[:, :, None], out_grad[0], jnp.zeros((), out_grad.dty...  7.02 us
    dot_general x1, matrix products, local(): lax.dot_general(factors, masked_grads, (((0,), (0,)), ((), ())), preferre...  6.63 us
    unnamed x7, local copies, waits for them, and re-layouts  5.56 us
  transfers between devices with their start and end apart: 6, of which 5 were waited for; matrix products, arithmetic and copies ran while one was open for 11% of the time, Pallas kernels for 0%

profile of v1, /device:TPU:4, one launch (start us, length us, event | category | flops | bytes accessed | tf_op | source)
XLA Modules:
  0.0 219.3 jit_solution(7451155161551556874)
XLA Ops:
  8.0 0.0 copy-start
  8.0 0.0 reduce-scatter.5.cloned.1.call-start
  8.1 1.0 fusion.6
  9.1 0.1 iota_compare_fusion
  9.2 2.5 %bitcast_select_fusion = bf16[1024,2048]{1,0:T(8,128)(2,1)S(1)} fusion(bf16[1,2,512,2048]{3,2,1,0:T(8,128)(2,1)} %param.8, pred[1024]{0:T(1024)(128)(4,1)S(1)} %lt.24), kind=kLoop, calls=%fused_computation | loop fusion | flops 2097152 | bytes 8389632 | tf_op jit(solution)/shard_map/jit(_where)/select_n | solution.py:59
  11.7 0.0 copy-done
  11.7 3.7 %fusion.9 = f32[1024,512]{1,0:T(8,128)} fusion(bf16[1024,2048]{1,0:T(8,128)(2,1)S(1)} %bitcast_select_fusion, bf16[512,2048]{1,0:T(8,128)(2,1)S(1)} %copy-done), kind=kOutput, calls=%fused_computation.14 | convolution fusion | flops 2147483648 | bytes 8388608 | tf_op jit(solution)/shard_map/dot_general | solution.py:62
  15.4 0.0 copy-start.1
  15.4 0.0 reduce-scatter.5.cloned.1.call-update
  15.5 0.0 all-gather.2.cloned.1.call-start
  15.5 39.4 %reduce-scatter.5.cloned.1.call-done = f32[128,512]{1,0:T(8,128)} async-done(((f32[1024,512]{1,0:T(8,128)}), f32[128,512]{1,0:T(8,128)}) %reduce-scatter.5.cloned.1.call-update) | async-done | bytes 262160 | tf_op jit(solution)/shard_map/reduce_scatter | solution.py:33
  55.0 0.0 all-gather.2.cloned.1.call-update
  55.0 0.0 copy-done.1
  55.0 0.1 copy.13
  55.2 1.1 broadcast_in_dim.45
  56.3 3.6 %all-to-all-start = ((bf16[8,1024,64]{1,2,0:T(8,128)(2,1)}), bf16[8,1024,64]{1,2,0:T(8,128)(2,1)S(1)}, u32[]{:S(2)}, u32[]{:S(2)}) async-start(bf16[8,1024,64]{1,2,0:T(8,128)(2,1)} %broadcast_in_dim.45), calls=%async_computation | async-start | bytes 2097152 | tf_op jit(solution)/shard_map/all_to_all | solution.py:9
  59.8 0.0 reduce-scatter.7.cloned.1.call-start
  59.9 4.5 %broadcast_select_fusion = bf16[1,2,512,2048]{3,2,1,0:T(8,128)(2,1)} fusion(bf16[1,2,512,2048]{3,2,1,0:T(8,128)(2,1)} %param.8, pred[2,512]{1,0:T(4,128)(4,1)S(1)} %iota_compare_fusion), kind=kLoop, calls=%fused_computation.1 | loop fusion | flops 2097152 | bytes 8389632 | tf_op jit(solution)/shard_map/jit(_where)/select_n | solution.py:59
  64.4 15.6 %all-to-all-done = bf16[8,1024,64]{1,2,0:T(8,128)(2,1)S(1)} async-done(((bf16[8,1024,64]{1,2,0:T(8,128)(2,1)}), bf16[8,1024,64]{1,2,0:T(8,128)(2,1)S(1)}, u32[]{:S(2)}, u32[]{:S(2)}) %all-to-all-start) | async-done | bytes 1048608 | tf_op jit(solution)/shard_map/all_to_all | solution.py:9
  80.0 6.6 %convolution_bitcast_fusion = f32[512,2048]{0,1:T(8,128)} fusion(bf16[1024,2048]{1,0:T(8,128)(2,1)} %bitcast.35, bf16[1024,512]{0,1:T(8,128)(2,1)S(1)} %bitcast.37), kind=kOutput, calls=%fused_computation.4 | convolution fusion | flops 2147483648 | bytes 9437184 | tf_op jit(solution)/shard_map/dot_general | solution.py:67
  86.6 5.4 %copy.18 = f32[512,2048]{1,0:T(8,128)} copy(f32[512,2048]{0,1:T(8,128)} %convolution_bitcast_fusion) | data formatting | bytes 8388608
  92.0 0.0 reduce-scatter.7.cloned.1.call-update
  92.0 0.0 all-gather.2.cloned.1.call-done
  92.1 3.4 %fusion.2 = f32[512,896]{1,0:T(8,128)S(1)} fusion(bf16[1024,896]{1,0:T(8,128)(2,1)} %bitcast.42, f32[1024,512]{1,0:T(8,128)} %all-gather.2.cloned.1.call-done), kind=kOutput, calls=%fused_computation.5 | convolution fusion | flops 940048384 | bytes 5767168 | tf_op jit(solution)/shard_map/dot_general | solution.py:76
  95.5 24.1 %all_to_all.20 = f32[4,896,128]{1,2,0:T(8,128)} all-to-all(f32[4,896,128]{1,2,0:T(8,128)S(1)} %bitcast.36), channel_id=1, replica_groups=mesh['mb'=8,'tp'=8,'dp'=4] {'dp'}, dimensions={0} | all-to-all | bytes 3670016 | tf_op jit(solution)/shard_map/all_to_all | solution.py:46
  119.5 27.1 %reduce-scatter.7.cloned.1.call-done = f32[64,2048]{1,0:T(8,128)} async-done(((f32[512,2048]{1,0:T(8,128)}), f32[64,2048]{1,0:T(8,128)}) %reduce-scatter.7.cloned.1.call-update) | async-done | bytes 524304 | tf_op jit(solution)/shard_map/reduce_scatter | solution.py:66
  146.7 4.8 %all-to-all-start.1 = ((f32[4,16,2048]{2,1,0:T(8,128)}), f32[4,16,2048]{2,1,0:T(8,128)S(1)}, u32[]{:S(2)}, u32[]{:S(2)}) async-start(f32[4,16,2048]{2,1,0:T(8,128)} %bitcast.39), calls=%async_computation.1 | async-start | bytes 1048576 | tf_op jit(solution)/shard_map/all_to_all | solution.py:46
  151.5 1.6 reduce_sum.29
  153.1 0.2 copy.15
  153.3 4.6 %all-to-all-done.1 = f32[4,16,2048]{2,1,0:T(8,128)S(1)} async-done(((f32[4,16,2048]{2,1,0:T(8,128)}), f32[4,16,2048]{2,1,0:T(8,128)S(1)}, u32[]{:S(2)}, u32[]{:S(2)}) %all-to-all-start.1) | async-done | bytes 524320 | tf_op jit(solution)/shard_map/all_to_all | solution.py:46
  157.9 1.5 stack.3
  159.4 4.4 %all-to-all-start.3 = ((bf16[8,1,896,128]{3,2,1,0:T(8,128)(2,1)}), bf16[8,1,896,128]{3,2,1,0:T(8,128)(2,1)}, u32[]{:S(2)}, u32[]{:S(2)}) async-start(bf16[8,1,896,128]{3,2,1,0:T(8,128)(2,1)} %stack.3), calls=%async_computation.4 | async-start | bytes 3670016 | tf_op jit(solution)/shard_map/all_to_all | solution.py:82
  163.7 0.7 reduce_sum.28
  164.4 43.9 %all-to-all-done.3 = bf16[8,1,896,128]{3,2,1,0:T(8,128)(2,1)} async-done(((bf16[8,1,896,128]{3,2,1,0:T(8,128)(2,1)}), bf16[8,1,896,128]{3,2,1,0:T(8,128)(2,1)}, u32[]{:S(2)}, u32[]{:S(2)}) %all-to-all-start.3) | async-done | bytes 1835040 | tf_op jit(solution)/shard_map/all_to_all | solution.py:82
  208.3 3.5 %fusion = f32[1,896,128]{2,0,1:T(1,128)} fusion(bf16[8,896,128]{2,1,0:T(8,128)(2,1)} %bitcast.13, s32[]{:T(128)S(6)} %axis_index.15), kind=kOutput, calls=%fused_computation.2 | convolution fusion | flops 1835016 | bytes 2293764 | tf_op jit(solution)/shard_map/k,kdr->dr/dot_general | solution.py:86
  (2 shorter events, 0.0 us)
Async XLA Ops:
  8.0 3.7 %copy-start = (bf16[512,2048]{1,0:T(8,128)(2,1)S(1)}, bf16[512,2048]{1,0:T(8,128)(2,1)}, u32[]{:S(2)}) copy-start(bf16[512,2048]{1,0:T(8,128)(2,1)} %param.9) | copy-start | bytes 6291460
  8.0 46.9 %reduce-scatter.5.cloned.1.call-start = ((), (), s32[]{:S(2)}) async-start(), calls=%async_computation.6 | async-start | bytes 2359296 | tf_op jit(solution)/shard_map/reduce_scatter | solution.py:33
  15.4 39.5 %copy-start.1 = (bf16[1,2,512,64]{2,3,1,0:T(8,128)(2,1)S(1)}, bf16[1,2,512,64]{2,3,1,0:T(8,128)(2,1)}, u32[]{:S(2)}) copy-start(bf16[1,2,512,64]{2,3,1,0:T(8,128)(2,1)} %param.7) | copy-start | bytes 393220
  15.5 76.6 %all-gather.2.cloned.1.call-start = ((), (), s32[]{:S(2)}) async-start(), calls=%async_computation.7 | async-start | bytes 2359296 | tf_op jit(solution)/shard_map/all_gather | solution.py:34
  56.3 23.7 %all-to-all-start = ((bf16[8,1024,64]{1,2,0:T(8,128)(2,1)}), bf16[8,1024,64]{1,2,0:T(8,128)(2,1)S(1)}, u32[]{:S(2)}, u32[]{:S(2)}) async-start(bf16[8,1024,64]{1,2,0:T(8,128)(2,1)} %broadcast_in_dim.45), calls=%async_computation | async-start | bytes 2097152 | tf_op jit(solution)/shard_map/all_to_all | solution.py:9
  59.8 86.9 %reduce-scatter.7.cloned.1.call-start = ((), (), s32[]{:S(2)}) async-start(), calls=%async_computation.8 | async-start | bytes 4718592 | tf_op jit(solution)/shard_map/reduce_scatter | solution.py:66
  146.7 11.2 %all-to-all-start.1 = ((f32[4,16,2048]{2,1,0:T(8,128)}), f32[4,16,2048]{2,1,0:T(8,128)S(1)}, u32[]{:S(2)}, u32[]{:S(2)}) async-start(f32[4,16,2048]{2,1,0:T(8,128)} %bitcast.39), calls=%async_computation.1 | async-start | bytes 1048576 | tf_op jit(solution)/shard_map/all_to_all | solution.py:46
  159.4 49.0 %all-to-all-start.3 = ((bf16[8,1,896,128]{3,2,1,0:T(8,128)(2,1)}), bf16[8,1,896,128]{3,2,1,0:T(8,128)(2,1)}, u32[]{:S(2)}, u32[]{:S(2)}) async-start(bf16[8,1,896,128]{3,2,1,0:T(8,128)(2,1)} %stack.3), calls=%async_computation.4 | async-start | bytes 3670016 | tf_op jit(solution)/shard_map/all_to_all | solution.py:82
Sparse Core Ops, SparseCore 0:
  15.6 39.3 reduce-scatter.4
  56.8 28.7 all-gather.1
Sparse Core Ops, SparseCore 1:
  92.1 54.5 reduce-scatter.6
